TPU v7x, 32 devices: a whole 2x2x4 slice. The times are simulated.
32 devices in a mesh: cuts: 4 (over z), dev: 8 (over y, x, core).
Axes of the slice: x: 2, y: 2, z: 4, core: 2. Of those that a mesh axis runs over, the one named last changes fastest.
Arguments:
- inputs: bfloat16 [16384, 3072], P(('cuts', 'dev')), may hold values from -6 to 6
- cotangent: bfloat16 [16384, 512], P(('cuts', 'dev')), may hold values from -0.29882812 to 0.29882812
- errors: bfloat16 [32, 3072, 512], P(('cuts', 'dev')), may hold values from -6 to 6
- previous_q: float32 [512, 64], replicated, may hold values from -0.25 to 0.25
Outputs:
- new_errors: bfloat16 [32, 3072, 512], P(('cuts', 'dev'))
- p_hat: float32 [3072, 64], replicated
- q_mean: float32 [512, 64], replicated
All inputs are finite; a program needn't handle non-finite values.
Results may differ from a plain program's by a relative error of at most 0.001.
Values sent between devices are 32-bit elements; how exact they have to be, the bound alone decides.
No kernel may reach another device: no remote copies, remote signals or barrier semaphores. Data moves between devices by JAX's collectives and lax.ppermute only.
A program may use at most 64 MiB of HBM per device.

v0:
```python
import jax
import jax.numpy as jnp
from jax import lax
from jax.sharding import PartitionSpec as P

HI = lax.Precision.HIGHEST


def solve_factor(gram, p_rows):
    lower = jnp.linalg.cholesky(gram)
    return lax.linalg.triangular_solve(lower, p_rows, left_side=False, lower=True, transpose_a=True)


def contract_rows(left, right):
    return lax.dot_general(
        left, right, (((0,), (0,)), ((), ())), precision=HI, preferred_element_type=jnp.float32
    )


def body(inputs, cotangent, errors, previous_q):
    grad = lax.dot_general(
        inputs, cotangent, (((0,), (0,)), ((), ())), preferred_element_type=jnp.float32
    )
    merged = grad + errors[0].astype(jnp.float32)
    devices = lax.axis_size("cuts") * lax.axis_size("dev")
    p_share = lax.psum_scatter(
        jnp.dot(merged, previous_q, precision=HI), "dev", scatter_dimension=0, tiled=True
    )
    p_share = lax.psum(p_share, "cuts")
    gram = lax.psum(contract_rows(p_share, p_share), "dev")
    hat_share = solve_factor(gram, p_share)
    p_hat = lax.all_gather(hat_share, "dev", axis=0, tiled=True)
    q_share = lax.psum_scatter(contract_rows(merged, p_hat), "dev", scatter_dimension=0, tiled=True)
    q_share = lax.psum(q_share, "cuts")
    q_sum = lax.all_gather(q_share, "dev", axis=0, tiled=True)
    q_mean = q_sum / devices
    approx = jnp.dot(p_hat, q_mean.T, precision=HI)
    new_errors = (merged - approx).astype(jnp.bfloat16)[None]
    return (new_errors, p_hat, q_mean)


def solution(mesh):
    in_specs = (
        P(("cuts", "dev"), None),
        P(("cuts", "dev"), None),
        P(("cuts", "dev"), None, None),
        P(),
    )
    out_specs = (P(("cuts", "dev"), None, None), P(), P())
    return jax.shard_map(body, mesh=mesh, in_specs=in_specs, out_specs=out_specs, check_vma=False)
```

profile of v0, /device:TPU:0, one launch (start us, length us, event | category | flops | bytes accessed | tf_op | source)
XLA Modules:
  0.0 238.6 jit_solution(2747192408776111508)
XLA Ops:
  7.2 0.0 copy-start
  7.2 0.0 copy-start.3
  7.2 0.0 reduce-scatter.3.cloned.1.call-start
  7.2 1.8 copy-done
  9.1 4.0 %convert_add_fusion = f32[3072,512]{1,0:T(8,128)S(1)} fusion(bf16[512,3072]{1,0:T(8,128)(2,1)S(1)} %copy-done, bf16[512,512]{1,0:T(8,128)(2,1)} %param.5, bf16[1,3072,512]{2,1,0:T(8,128)(2,1)} %param.6), kind=kOutput, calls=%fused_computation | convolution fusion | flops 1613758464 | bytes 13107200 | tf_op jit(solution)/shard_map/dot_general | solution.py:21
  13.0 0.0 copy-start.1
  13.1 2.7 %copy-done.1 = f32[3072,512]{1,0:T(8,128)} copy-done((f32[3072,512]{1,0:T(8,128)}, f32[3072,512]{1,0:T(8,128)S(1)}, u32[]{:S(2)}) %copy-start.1) | copy-done | bytes 6291480
  15.7 0.0 copy-done.3
  15.7 7.1 %fusion.5 = f32[3072,64]{0,1:T(8,128)} fusion(f32[3072,512]{1,0:T(8,128)S(1)} %convert_add_fusion, f32[512,64]{0,1:T(8,128)S(1)} %copy-done.3), kind=kOutput, calls=%fused_computation.14 | convolution fusion | flops 1207959552 | bytes 7208960 | tf_op jit(solution)/shard_map/dot_general | solution.py:27
  22.8 0.0 reduce-scatter.3.cloned.1.call-update
  22.8 0.0 all-reduce.2.cloned.1.call-start
  22.9 37.8 %reduce-scatter.3.cloned.1.call-done = f32[384,64]{0,1:T(8,128)} async-done(((f32[3072,64]{0,1:T(8,128)}), f32[384,64]{0,1:T(8,128)}) %reduce-scatter.3.cloned.1.call-update) | async-done | bytes 98320 | tf_op jit(solution)/shard_map/reduce_scatter | solution.py:26
  60.6 0.0 all-reduce.2.cloned.1.call-update
  60.7 0.0 reduce-scatter.5.cloned.1.call-start
  60.7 36.7 %all-reduce.2.cloned.1.call-done = f32[384,64]{0,1:T(8,128)} async-done(((f32[384,64]{0,1:T(8,128)}), f32[384,64]{0,1:T(8,128)}) %all-reduce.2.cloned.1.call-update) | async-done | bytes 98320 | tf_op jit(solution)/shard_map/psum | solution.py:29
  97.4 1.2 fusion.6
  98.7 22.4 %psum.22 = f32[64,64]{0,1:T(8,128)S(1)} all-reduce(f32[64,64]{0,1:T(8,128)S(1)} %fusion.6), channel_id=1, replica_groups=mesh['cuts'=4,'dev'=8] {'dev'}, use_global_device_ids=true, to_apply=%region_2.0 | all-reduce | flops 4096 | bytes 32768 | tf_op jit(solution)/shard_map/psum | solution.py:30
  121.0 0.1 copy.8
  121.1 5.8 %cholesky.16 = f32[64,64]{1,0:T(8,128)S(1)} custom-call(f32[64,64]{1,0:T(8,128)S(1)} %fusion.4), custom_call_target="Cholesky" | custom-call | tf_op jit(solution)/shard_map/jit(cholesky)/cholesky | solution.py:10
  127.0 0.6 compare_reduce_fusion
  127.6 0.7 fusion.1
  128.3 4.9 %custom-call.6 = f32[1,64,64]{1,2,0:T(8,128)S(1)} custom-call(f32[1,64,64]{2,1,0:T(8,128)S(1)} %fusion.1), custom_call_target="InvertDiagBlocksLowerTriangular" | custom-call | tf_op jit(solution)/shard_map/triangular_solve | solution.py:11
  133.2 1.2 fusion.2
  134.4 11.1 %all_gather.6 = f32[3072,64]{0,1:T(8,128)S(1)} all-gather(f32[384,64]{0,1:T(8,128)S(1)} %fusion.2), channel_id=1, replica_groups=mesh['cuts'=4,'dev'=8] {'dev'}, dimensions={0}, use_global_device_ids=true | all-gather | bytes 884736 | tf_op jit(solution)/shard_map/all_gather | solution.py:32
  145.5 0.0 copy-start.2
  145.5 0.9 copy-done.2
  146.4 12.7 %fusion.7 = f32[512,64]{1,0:T(8,128)} fusion(f32[3072,512]{1,0:T(8,128)} %copy-done.1, f32[3072,64]{0,1:T(8,128)S(1)} %all_gather.6), kind=kOutput, calls=%fused_computation.16 | convolution fusion | flops 1207959552 | bytes 7208960 | tf_op jit(solution)/shard_map/dot_general | solution.py:15
  159.1 0.0 reduce-scatter.5.cloned.1.call-update
  159.1 32.7 %reduce-scatter.5.cloned.1.call-done = f32[64,64]{1,0:T(8,128)} async-done(((f32[512,64]{1,0:T(8,128)}), f32[64,64]{1,0:T(8,128)}) %reduce-scatter.5.cloned.1.call-update) | async-done | bytes 16400 | tf_op jit(solution)/shard_map/reduce_scatter | solution.py:33
  191.8 19.6 %psum.23 = f32[64,64]{1,0:T(8,128)S(1)} all-reduce(f32[64,64]{1,0:T(8,128)} %reduce-scatter.5.cloned.1.call-done), channel_id=1, replica_groups=mesh['cuts'=4,'dev'=8] {'cuts'}, use_global_device_ids=true, to_apply=%region_6.7 | all-reduce | flops 4096 | bytes 32768 | tf_op jit(solution)/shard_map/psum | solution.py:34
  211.4 9.2 %all_gather.7 = f32[512,64]{1,0:T(8,128)S(1)} all-gather(f32[64,64]{1,0:T(8,128)S(1)} %psum.23), channel_id=1, replica_groups=mesh['cuts'=4,'dev'=8] {'dev'}, dimensions={0}, use_global_device_ids=true | all-gather | bytes 147456 | tf_op jit(solution)/shard_map/all_gather | solution.py:35
  220.6 8.6 %fusion = bf16[1,3072,512]{2,1,0:T(8,128)(2,1)} fusion(f32[3072,512]{1,0:T(8,128)} %copy-done.1, f32[3072,64]{0,1:T(8,128)} %copy-done.2, f32[512,64]{1,0:T(8,128)S(1)} %all_gather.7), kind=kOutput, calls=%fused_computation.2 | convolution fusion | flops 1211138048 | bytes 10354688 | tf_op jit(solution)/shard_map/dot_general | solution.py:37
  229.2 0.8 copy.9
  230.0 2.1 copy.13
  (3 shorter events, 0.1 us)
Async XLA Ops:
  7.2 1.9 copy-start
  7.2 8.5 %copy-start.3 = (f32[512,64]{0,1:T(8,128)S(1)}, f32[512,64]{0,1:T(8,128)}, u32[]{:S(2)}) copy-start(f32[512,64]{0,1:T(8,128)} %param.7) | copy-start | bytes 393220
  7.2 53.5 %reduce-scatter.3.cloned.1.call-start = ((), (), s32[]{:S(2)}) async-start(), calls=%async_computation.2 | async-start | bytes 884736 | tf_op jit(solution)/shard_map/reduce_scatter | solution.py:26
  13.0 2.7 %copy-start.1 = (f32[3072,512]{1,0:T(8,128)}, f32[3072,512]{1,0:T(8,128)S(1)}, u32[]{:S(2)}) copy-start(f32[3072,512]{1,0:T(8,128)S(1)} %convert_add_fusion) | copy-start | bytes 18874372
  22.8 74.6 %all-reduce.2.cloned.1.call-start = ((), (), s32[]{:S(2)}) async-start(), calls=%async_computation.3 | async-start | bytes 196608 | tf_op jit(solution)/shard_map/psum | solution.py:29
  60.7 131.1 %reduce-scatter.5.cloned.1.call-start = ((), (), s32[]{:S(2)}) async-start(), calls=%async_computation.4 | async-start | bytes 294912 | tf_op jit(solution)/shard_map/reduce_scatter | solution.py:33
  145.5 0.9 copy-start.2
Sparse Core Ops, SparseCore 0:
  22.9 37.6 reduce-scatter.2
  63.0 34.4 all-reduce.1
  159.2 32.5 reduce-scatter.4
where the time goes:
time: 239 us
  waiting for transfers between devices  107 us (45%)
  blocking collectives  62.3 us (26%)
  matrix products  34.7 us (15%)
  between operations  13.8 us (6%)
  other arithmetic  12.1 us (5%)
  local copies, waits for them, and re-layouts  8.29 us (3%)
    reduce_scatter x1, waiting for transfers between devices, body(): lax.psum_scatter(jnp.dot(merged, previous_q, precision=HI), 'dev', scatte...  37.8 us
    psum x1, waiting for transfers between devices, body(): p_share = lax.psum(p_share, 'cuts')  36.7 us
    reduce_scatter x1, waiting for transfers between devices, body(): lax.psum_scatter(contract_rows(merged, p_hat), 'dev', scatter_dimension=0...  32.7 us
    psum x1, blocking collectives, body(): gram = lax.psum(contract_rows(p_share, p_share), 'dev')  22.4 us
    psum x1, blocking collectives, body(): q_share = lax.psum(q_share, 'cuts')  19.6 us
    dot_general x2, matrix products, contract_rows(): lax.dot_general(left, right, (((0,), (0,)), ((), ())), precision=HI, pref...  13.9 us
    all_gather x1, blocking collectives, body(): p_hat = lax.all_gather(hat_share, 'dev', axis=0, tiled=True)  11.1 us
    all_gather x1, blocking collectives, body(): q_sum = lax.all_gather(q_share, 'dev', axis=0, tiled=True)  9.24 us
  transfers between devices with their start and end apart: 3, of which 3 were waited for; matrix products, arithmetic and copies ran while one was open for 0% of the time, Pallas kernels for 0%

commit v1 on v0

--- a/solution.py
+++ b/solution.py
@@ -31,7 +31,7 @@
     hat_share = solve_factor(gram, p_share)
     p_hat = lax.all_gather(hat_share, "dev", axis=0, tiled=True)
     q_share = lax.psum_scatter(contract_rows(merged, p_hat), "dev", scatter_dimension=0, tiled=True)
-    q_share = lax.psum(q_share, "cuts")
+    q_share = jnp.sum(lax.all_gather(q_share, "cuts"), axis=0)
     q_sum = lax.all_gather(q_share, "dev", axis=0, tiled=True)
     q_mean = q_sum / devices
     approx = jnp.dot(p_hat, q_mean.T, precision=HI)

time: 239 us -> 233 us (0.975)
  blocking collectives: 62.3 us -> 56.4 us
    psum x1 -> x0, blocking collectives: 19.6 us -> none  [body(): q_share = lax.psum(q_share, 'cuts')]
    all_gather x0 -> x1, blocking collectives: none -> 13.6 us  [body(): q_share = jnp.sum(lax.all_gather(q_share, 'cuts'), axis=0)]
where the time goes in v1:
time: 233 us
  waiting for transfers between devices  107 us (46%)
  blocking collectives  56.4 us (24%)
  matrix products  34.7 us (15%)
  between operations  13.8 us (6%)
  other arithmetic  12.1 us (5%)
  local copies, waits for them, and re-layouts  8.29 us (4%)
    reduce_scatter x1, waiting for transfers between devices, body(): lax.psum_scatter(jnp.dot(merged, previous_q, precision=HI), 'dev', scatte...  37.8 us
    psum x1, waiting for transfers between devices, body(): p_share = lax.psum(p_share, 'cuts')  36.7 us
    reduce_scatter x1, waiting for transfers between devices, body(): lax.psum_scatter(contract_rows(merged, p_hat), 'dev', scatter_dimension=0...  32.7 us
    psum x1, blocking collectives, body(): gram = lax.psum(contract_rows(p_share, p_share), 'dev')  22.4 us
    dot_general x2, matrix products, contract_rows(): lax.dot_general(left, right, (((0,), (0,)), ((), ())), precision=HI, pref...  13.9 us
    all_gather x1, blocking collectives, body(): q_share = jnp.sum(lax.all_gather(q_share, 'cuts'), axis=0)  13.6 us
    all_gather x1, blocking collectives, body(): p_hat = lax.all_gather(hat_share, 'dev', axis=0, tiled=True)  11.1 us
    all_gather x1, blocking collectives, body(): q_sum = lax.all_gather(q_share, 'dev', axis=0, tiled=True)  9.35 us
  transfers between devices with their start and end apart: 3, of which 3 were waited for; matrix products, arithmetic and copies ran while one was open for 0% of the time, Pallas kernels for 0%

profile of v1, /device:TPU:0, one launch (start us, length us, event | category | flops | bytes accessed | tf_op | source)
XLA Modules:
  0.0 232.7 jit_solution(7722686916687195156)
XLA Ops:
  7.2 0.0 copy-start
  7.2 0.0 copy-start.3
  7.2 0.0 reduce-scatter.3.cloned.1.call-start
  7.2 1.8 copy-done
  9.1 4.0 %convert_add_fusion = f32[3072,512]{1,0:T(8,128)S(1)} fusion(bf16[512,3072]{1,0:T(8,128)(2,1)S(1)} %copy-done, bf16[512,512]{1,0:T(8,128)(2,1)} %param.5, bf16[1,3072,512]{2,1,0:T(8,128)(2,1)} %param.6), kind=kOutput, calls=%fused_computation | convolution fusion | flops 1613758464 | bytes 13107200 | tf_op jit(solution)/shard_map/dot_general | solution.py:21
  13.0 0.0 copy-start.1
  13.1 2.7 %copy-done.1 = f32[3072,512]{1,0:T(8,128)} copy-done((f32[3072,512]{1,0:T(8,128)}, f32[3072,512]{1,0:T(8,128)S(1)}, u32[]{:S(2)}) %copy-start.1) | copy-done | bytes 6291480
  15.7 0.0 copy-done.3
  15.7 7.1 %fusion.5 = f32[3072,64]{0,1:T(8,128)} fusion(f32[3072,512]{1,0:T(8,128)S(1)} %convert_add_fusion, f32[512,64]{0,1:T(8,128)S(1)} %copy-done.3), kind=kOutput, calls=%fused_computation.14 | convolution fusion | flops 1207959552 | bytes 7208960 | tf_op jit(solution)/shard_map/dot_general | solution.py:27
  22.8 0.0 reduce-scatter.3.cloned.1.call-update
  22.8 0.0 all-reduce.2.cloned.1.call-start
  22.9 37.8 %reduce-scatter.3.cloned.1.call-done = f32[384,64]{0,1:T(8,128)} async-done(((f32[3072,64]{0,1:T(8,128)}), f32[384,64]{0,1:T(8,128)}) %reduce-scatter.3.cloned.1.call-update) | async-done | bytes 98320 | tf_op jit(solution)/shard_map/reduce_scatter | solution.py:26
  60.6 0.0 all-reduce.2.cloned.1.call-update
  60.7 0.0 reduce-scatter.5.cloned.1.call-start
  60.7 36.7 %all-reduce.2.cloned.1.call-done = f32[384,64]{0,1:T(8,128)} async-done(((f32[384,64]{0,1:T(8,128)}), f32[384,64]{0,1:T(8,128)}) %all-reduce.2.cloned.1.call-update) | async-done | bytes 98320 | tf_op jit(solution)/shard_map/psum | solution.py:29
  97.4 1.2 fusion.6
  98.7 22.4 %psum.15 = f32[64,64]{0,1:T(8,128)S(1)} all-reduce(f32[64,64]{0,1:T(8,128)S(1)} %fusion.6), channel_id=1, replica_groups=mesh['cuts'=4,'dev'=8] {'dev'}, use_global_device_ids=true, to_apply=%region_2.0 | all-reduce | flops 4096 | bytes 32768 | tf_op jit(solution)/shard_map/psum | solution.py:30
  121.0 0.1 copy.10
  121.1 5.8 %cholesky.16 = f32[64,64]{1,0:T(8,128)S(1)} custom-call(f32[64,64]{1,0:T(8,128)S(1)} %fusion.4), custom_call_target="Cholesky" | custom-call | tf_op jit(solution)/shard_map/jit(cholesky)/cholesky | solution.py:10
  127.0 0.6 compare_reduce_fusion
  127.6 0.7 fusion.1
  128.3 4.9 %custom-call.6 = f32[1,64,64]{1,2,0:T(8,128)S(1)} custom-call(f32[1,64,64]{2,1,0:T(8,128)S(1)} %fusion.1), custom_call_target="InvertDiagBlocksLowerTriangular" | custom-call | tf_op jit(solution)/shard_map/triangular_solve | solution.py:11
  133.2 1.2 fusion.2
  134.4 11.1 %all_gather.12 = f32[3072,64]{0,1:T(8,128)S(1)} all-gather(f32[384,64]{0,1:T(8,128)S(1)} %fusion.2), channel_id=1, replica_groups=mesh['cuts'=4,'dev'=8] {'dev'}, dimensions={0}, use_global_device_ids=true | all-gather | bytes 884736 | tf_op jit(solution)/shard_map/all_gather | solution.py:32
  145.5 0.0 copy-start.2
  145.5 0.9 copy-done.2
  146.4 12.7 %fusion.7 = f32[512,64]{1,0:T(8,128)} fusion(f32[3072,512]{1,0:T(8,128)} %copy-done.1, f32[3072,64]{0,1:T(8,128)S(1)} %all_gather.12), kind=kOutput, calls=%fused_computation.16 | convolution fusion | flops 1207959552 | bytes 7208960 | tf_op jit(solution)/shard_map/dot_general | solution.py:15
  159.1 0.0 reduce-scatter.5.cloned.1.call-update
  159.1 32.7 %reduce-scatter.5.cloned.1.call-done = f32[64,64]{1,0:T(8,128)} async-done(((f32[512,64]{1,0:T(8,128)}), f32[64,64]{1,0:T(8,128)}) %reduce-scatter.5.cloned.1.call-update) | async-done | bytes 16400 | tf_op jit(solution)/shard_map/reduce_scatter | solution.py:33
  191.8 13.6 %all-gather = f32[256,64]{1,0:T(8,128)S(1)} all-gather(f32[64,64]{1,0:T(8,128)} %reduce-scatter.5.cloned.1.call-done), channel_id=2, replica_groups=mesh['cuts'=4,'dev'=8] {'cuts'}, dimensions={0}, use_global_device_ids=true | all-gather | bytes 81920 | tf_op jit(solution)/shard_map/all_gather | solution.py:34
  205.4 9.4 %all_gather.15 = f32[512,64]{1,0:T(8,128)S(1)} all-gather(f32[64,64]{1,0:T(8,128)S(1)} %reduce_sum.9), channel_id=1, replica_groups=mesh['cuts'=4,'dev'=8] {'dev'}, dimensions={0}, use_global_device_ids=true | all-gather | bytes 147456 | tf_op jit(solution)/shard_map/all_gather | solution.py:35
  214.7 8.6 %fusion = bf16[1,3072,512]{2,1,0:T(8,128)(2,1)} fusion(f32[3072,512]{1,0:T(8,128)} %copy-done.1, f32[3072,64]{0,1:T(8,128)} %copy-done.2, f32[512,64]{1,0:T(8,128)S(1)} %all_gather.15), kind=kOutput, calls=%fused_computation.2 | convolution fusion | flops 1211138048 | bytes 10354688 | tf_op jit(solution)/shard_map/dot_general | solution.py:37
  223.3 0.8 copy.11
  224.1 2.1 copy.15
  (4 shorter events, 0.1 us)
Async XLA Ops:
  7.2 1.9 copy-start
  7.2 8.5 %copy-start.3 = (f32[512,64]{0,1:T(8,128)S(1)}, f32[512,64]{0,1:T(8,128)}, u32[]{:S(2)}) copy-start(f32[512,64]{0,1:T(8,128)} %param.7) | copy-start | bytes 393220
  7.2 53.5 %reduce-scatter.3.cloned.1.call-start = ((), (), s32[]{:S(2)}) async-start(), calls=%async_computation.2 | async-start | bytes 884736 | tf_op jit(solution)/shard_map/reduce_scatter | solution.py:26
  13.0 2.7 %copy-start.1 = (f32[3072,512]{1,0:T(8,128)}, f32[3072,512]{1,0:T(8,128)S(1)}, u32[]{:S(2)}) copy-start(f32[3072,512]{1,0:T(8,128)S(1)} %convert_add_fusion) | copy-start | bytes 18874372
  22.8 74.6 %all-reduce.2.cloned.1.call-start = ((), (), s32[]{:S(2)}) async-start(), calls=%async_computation.3 | async-start | bytes 196608 | tf_op jit(solution)/shard_map/psum | solution.py:29
  60.7 131.1 %reduce-scatter.5.cloned.1.call-start = ((), (), s32[]{:S(2)}) async-start(), calls=%async_computation.4 | async-start | bytes 294912 | tf_op jit(solution)/shard_map/reduce_scatter | solution.py:33
  145.5 0.9 copy-start.2
Sparse Core Ops, SparseCore 0:
  22.9 37.6 reduce-scatter.2
  63.0 34.4 all-reduce.1
  159.2 32.5 reduce-scatter.4
